TPU v7x, 32 devices: a whole 2x2x4 slice. The times are simulated.
32 devices in a mesh: fsdp: 16 (over z, y, core), tp: 2 (over x).
Axes of the slice: x: 2, y: 2, z: 4, core: 2. Of those that a mesh axis runs over, the one named last changes fastest.
Arguments:
- tokens: bfloat16 [6144, 5632], P('fsdp', 'tp'), may hold values from -6 to 6
- gain: float32 [5632], replicated, may hold values from 0.1 to 1.9
- query_projection_weight: bfloat16 [5632, 6144], P('fsdp', 'tp'), may hold values from -0.078125 to 0.078125
- key_projection_weight: bfloat16 [5632, 1024], P('fsdp', 'tp'), may hold values from -0.078125 to 0.078125
- value_projection_weight: bfloat16 [5632, 1024], P('fsdp', 'tp'), may hold values from -0.078125 to 0.078125
- adapter_down_factors: bfloat16 [3, 16, 5632], replicated, may hold values from -0.078125 to 0.078125
- query_adapter_up: bfloat16 [16, 6144], P(None, 'tp'), may hold values from -0.078125 to 0.078125
- key_adapter_up: bfloat16 [16, 1024], P(None, 'tp'), may hold values from -0.1875 to 0.1875
- value_adapter_up: bfloat16 [16, 1024], P(None, 'tp'), may hold values from -0.1875 to 0.1875
- query_cotangent: bfloat16 [6144, 6144], P('fsdp', 'tp'), may hold values from -6 to 6
- key_cotangent: bfloat16 [6144, 1024], P('fsdp', 'tp'), may hold values from -6 to 6
- value_cotangent: bfloat16 [6144, 1024], P('fsdp', 'tp'), may hold values from -6 to 6
Outputs:
- grad_tokens: bfloat16 [6144, 5632], P('fsdp', 'tp')
- grad_down: float32 [3, 16, 5632], P(None, None, 'tp')
- grad_up_query: float32 [16, 6144], P(None, 'tp')
- grad_up_key: float32 [16, 1024], P(None, 'tp')
- grad_up_value: float32 [16, 1024], P(None, 'tp')
All inputs are finite; a program needn't handle non-finite values.
Results may differ from a plain program's by a relative error of at most 0.0096.
Values may be sent and summed in bfloat16 or wider, within the bound.
A program may use at most 128 MiB of HBM per device.

v0:
```python
import math

import jax
import jax.numpy as jnp
from jax import lax
from jax.sharding import PartitionSpec as P

norm_eps = 1e-05
adapter_scale = 2.0


def transposed_product(cotangent, piece):
    return lax.dot_general(
        cotangent, piece, (((1,), (1,)), ((), ())), preferred_element_type=jnp.float32
    )


def shards(
    tokens,
    gain,
    query_projection_weight,
    key_projection_weight,
    value_projection_weight,
    adapter_down_factors,
    query_adapter_up,
    key_adapter_up,
    value_adapter_up,
    query_cotangent,
    key_cotangent,
    value_cotangent,
):
    adapter_up_factors = (query_adapter_up, key_adapter_up, value_adapter_up)
    cotangent_list = (query_cotangent, key_cotangent, value_cotangent)
    tensor_slice_index = lax.axis_index("tp")
    number_of_rows, owned_width = tokens.shape
    full_width = gain.shape[0]
    token_width_matrix = tokens.astype(jnp.float32)
    gain_own = lax.dynamic_slice_in_dim(gain, tensor_slice_index * owned_width, owned_width, 0)
    down_owned_slice = lax.dynamic_slice_in_dim(
        adapter_down_factors, tensor_slice_index * owned_width, owned_width, 2
    )
    scaled_part = token_width_matrix * gain_own[None, :]
    adapter_input_slice = jnp.einsum(
        "td,krd->ktr",
        scaled_part,
        down_owned_slice.astype(jnp.float32),
        precision=lax.Precision.HIGHEST,
    )
    adapter_output_slice = jnp.stack(
        [
            jnp.dot(
                cotangent_list[slice_member],
                adapter_up_factors[slice_member].T,
                preferred_element_type=jnp.float32,
            )
            for slice_member in range(3)
        ]
    )
    squared_total, adapter_input_unnormed, adapter_output = lax.psum(
        (
            jnp.sum(token_width_matrix * token_width_matrix, axis=1),
            adapter_input_slice,
            adapter_output_slice,
        ),
        "tp",
    )
    inverse_root_mean = lax.rsqrt(squared_total / full_width + norm_eps)[:, None]
    adapter_input = adapter_input_unnormed * inverse_root_mean[None]
    unit_rows = token_width_matrix * inverse_root_mean
    normed = (unit_rows * gain_own[None, :]).astype(jnp.bfloat16)
    input_lowrank = adapter_input.astype(jnp.bfloat16)
    output_lowrank = adapter_output.astype(jnp.bfloat16)
    gradient_scale = adapter_scale / math.sqrt(number_of_rows * lax.axis_size("fsdp"))
    down_local = gradient_scale * jnp.einsum(
        "ktr,td->krd", output_lowrank, normed, preferred_element_type=jnp.float32
    )
    up_local = tuple(
        (
            gradient_scale
            * jnp.dot(
                input_lowrank[slice_member].T,
                cotangent_list[slice_member],
                preferred_element_type=jnp.float32,
            )
            for slice_member in range(3)
        )
    )
    grad_down, grad_up_query, grad_up_key, grad_up_value = lax.psum(
        (down_local, up_local[0], up_local[1], up_local[2]), "fsdp"
    )
    empty = jnp.zeros((number_of_rows, full_width), jnp.float32)

    def adder(cotangent, total, piece):
        return total + transposed_product(cotangent, piece)

    partial_back = adder(
        query_cotangent, empty, lax.all_gather(query_projection_weight, "fsdp", axis=0, tiled=True)
    )
    partial_back = adder(
        key_cotangent,
        partial_back,
        lax.all_gather(key_projection_weight, "fsdp", axis=0, tiled=True),
    )
    partial_back = adder(
        value_cotangent,
        partial_back,
        lax.all_gather(value_projection_weight, "fsdp", axis=0, tiled=True),
    )
    backward_result = lax.psum_scatter(partial_back, "tp", scatter_dimension=1, tiled=True)
    backward_result = backward_result + adapter_scale * jnp.einsum(
        "ktr,krd->td", output_lowrank, down_owned_slice, preferred_element_type=jnp.float32
    )
    gained = gain_own[None, :] * backward_result
    inner = lax.psum(jnp.sum(gained * unit_rows, axis=1), "tp") / full_width
    grad_tokens = (inverse_root_mean * (gained - unit_rows * inner[:, None])).astype(jnp.bfloat16)
    return (grad_tokens, grad_down, grad_up_query, grad_up_key, grad_up_value)


def solution(mesh):
    in_specs = (
        P("fsdp", "tp"),
        P(),
        P("fsdp", "tp"),
        P("fsdp", "tp"),
        P("fsdp", "tp"),
        P(),
        P(None, "tp"),
        P(None, "tp"),
        P(None, "tp"),
        P("fsdp", "tp"),
        P("fsdp", "tp"),
        P("fsdp", "tp"),
    )
    out_specs = (P("fsdp", "tp"), P(None, None, "tp"), P(None, "tp"), P(None, "tp"), P(None, "tp"))
    return jax.shard_map(shards, mesh=mesh, in_specs=in_specs, out_specs=out_specs, check_vma=False)
```

profile of v0, /device:TPU:0, one launch (start us, length us, event | category | flops | bytes accessed | tf_op | source)
XLA Modules:
  0.0 531.9 jit_solution(16728391225981256353)
XLA Ops:
  8.1 0.7 all-gather.4.cloned.1.call-update
  8.8 0.7 all-gather.6.cloned.1.call-update
  9.5 0.7 all-gather.8.cloned.1.call-update
  10.3 0.8 dynamic_slice.6
  11.1 4.8 fusion.20
  16.0 170.1 %all-gather.4.cloned.1.call-done = bf16[5632,3072]{1,0:T(8,128)(2,1)} async-done(((bf16[352,3072]{1,0:T(8,128)(2,1)}), bf16[5632,3072]{1,0:T(8,128)(2,1)}) %all-gather.4.cloned.1.call-update) | async-done | bytes 34603024 | tf_op jit(solution)/shard_map/all_gather | solution.py:97
  186.2 21.3 %fusion.29 = f32[384,5632]{1,0:T(8,128)} fusion(bf16[384,3072]{1,0:T(8,128)(2,1)S(1)} %copy-done, bf16[5632,3072]{1,0:T(8,128)(2,1)} %all-gather.4.cloned.1.call-done), kind=kOutput, calls=%fused_computation.45 | convolution fusion | flops 13287555072 | bytes 45613056 | tf_op jit(solution)/shard_map/dot_general | solution.py:13
  207.4 39.7 %all-gather.6.cloned.1.call-done = bf16[5632,512]{1,0:T(8,128)(2,1)} async-done(((bf16[352,512]{1,0:T(8,128)(2,1)}), bf16[5632,512]{1,0:T(8,128)(2,1)}) %all-gather.6.cloned.1.call-update) | async-done | bytes 5767184 | tf_op jit(solution)/shard_map/all_gather | solution.py:102
  247.1 11.0 %convolution_add_fusion.1 = f32[384,5632]{1,0:T(8,128)} fusion(f32[384,5632]{1,0:T(8,128)} %fusion.29, bf16[384,512]{1,0:T(8,128)(2,1)S(1)} %copy-done.3, bf16[5632,512]{1,0:T(8,128)(2,1)} %all-gather.6.cloned.1.call-done), kind=kOutput, calls=%fused_computation.1 | convolution fusion | flops 2216755200 | bytes 23461888 | tf_op jit(solution)/shard_map/dot_general | solution.py:13
  258.1 48.7 %all-gather.8.cloned.1.call-done = bf16[5632,512]{1,0:T(8,128)(2,1)} async-done(((bf16[352,512]{1,0:T(8,128)(2,1)}), bf16[5632,512]{1,0:T(8,128)(2,1)}) %all-gather.8.cloned.1.call-update) | async-done | bytes 5767184 | tf_op jit(solution)/shard_map/all_gather | solution.py:107
  306.7 11.0 %convolution_add_fusion = f32[384,5632]{1,0:T(8,128)} fusion(f32[384,5632]{1,0:T(8,128)} %convolution_add_fusion.1, bf16[384,512]{1,0:T(8,128)(2,1)S(1)} %copy-done.2, bf16[5632,512]{1,0:T(8,128)(2,1)} %all-gather.8.cloned.1.call-done), kind=kOutput, calls=%fused_computation | convolution fusion | flops 2216755200 | bytes 23461888 | tf_op jit(solution)/shard_map/dot_general | solution.py:13
  317.8 0.6 copy-done.5
  318.7 0.3 convolution_bitcast_fusion.1
  318.9 0.7 convolution_bitcast_fusion.3
  319.7 0.4 copy-done.1
  320.1 0.5 fusion.11
  320.6 11.1 %all-reduce.2 = (bf16[3,384,16]{1,2,0:T(8,128)(2,1)S(1)}, f32[384]{0:T(512)S(1)}) all-reduce(f32[3,384,16]{1,2,0:T(8,128)S(1)} %pad_maximum_fusion, f32[384]{0:T(512)S(1)} %fusion.11), channel_id=1, replica_groups=mesh['fsdp'=16,'tp'=2] {'tp'}, use_global_device_ids=true, to_apply=%region_3.0 | all-reduce | flops 18816 | bytes 113664 | tf_op jit(solution)/shard_map/psum | solution.py:59
  331.7 3.2 convolution_multiply_fusion
  334.9 0.9 multiply_convert_fusion
  335.8 0.8 convolution_multiply_fusion.2
  336.6 0.8 convolution_multiply_fusion.3
  337.4 0.2 all-reduce.11.cloned.1.call-start
  337.6 1.1 convolution_multiply_fusion.1
  338.8 81.6 %reduce-scatter.2.cloned.1.call-done = f32[384,2816]{1,0:T(8,128)} async-done(((f32[384,5632]{1,0:T(8,128)}), f32[384,2816]{1,0:T(8,128)}) %reduce-scatter.2.cloned.1.call-update) | async-done | bytes 4325392 | tf_op jit(solution)/shard_map/reduce_scatter | solution.py:109
  420.4 6.2 %fusion.6 = (f32[384]{0:T(512)S(1)}, f32[384,2816]{1,0:T(8,128)}) fusion(bf16[384,2816]{1,0:T(8,128)(2,1)} %param.12, f32[384]{0:T(512)S(1)} %add_rsqrt_fusion, f32[384,2816]{1,0:T(8,128)} %reduce-scatter.2.cloned.1.call-done, bf16[3,384,16]{1,2,0:T(8,128)(2,1)S(1)} %get-tuple-element.9, bf16[3,16,5632]{2,1,0:T(8,128)(2,1)} %param.17, s32[]{:T(128)S(6)} %select_n.4, ...), kind=kOutput, calls=%fused_computation.12 | convolution fusion | flops 111378048 | bytes 11134980 | tf_op jit(solution)/shard_map/ktr,krd->td/dot_general | solution.py:110
  426.6 4.9 psum.58
  431.5 5.5 %fusion.9 = bf16[384,2816]{1,0:T(8,128)(2,1)} fusion(f32[384,2816]{1,0:T(8,128)} %get-tuple-element.12, bf16[384,2816]{1,0:T(8,128)(2,1)} %param.12, f32[384]{0:T(512)S(1)} %broadcast_multiply_fusion, f32[384]{0:T(512)S(1)} %add_rsqrt_fusion), kind=kLoop, calls=%fused_computation.15 | loop fusion | flops 6488064 | bytes 8653824 | tf_op jit(solution)/shard_map/convert_element_type | solution.py:115
  437.0 81.6 %all-reduce.11.cloned.1.call-done = (f32[3,16,2816]{2,1,0:T(8,128)}, f32[16,3072]{1,0:T(8,128)}) async-done(((f32[3,16,2816]{2,1,0:T(8,128)}, f32[16,3072]{1,0:T(8,128)}), (f32[3,16,2816]{2,1,0:T(8,128)}, f32[16,3072]{1,0:T(8,128)})) %all-reduce.11.cloned.1.call-update) | async-done | bytes 737296 | tf_op jit(solution)/shard_map/psum | solution.py:88
  518.6 1.9 copy.22
  520.4 1.6 copy.23
  522.0 1.4 copy.24
  523.4 1.4 copy.25
  (28 shorter events, 0.6 us)
Async XLA Ops:
  8.0 178.2 %copy-start = (bf16[384,3072]{1,0:T(8,128)(2,1)S(1)}, bf16[384,3072]{1,0:T(8,128)(2,1)}, u32[]{:S(2)}) copy-start(bf16[384,3072]{1,0:T(8,128)(2,1)} %param.21) | copy-start | bytes 7077892
  8.0 178.1 %all-gather.4.cloned.1.call-start = ((), (), s32[]{:S(2)}) async-start(), calls=%async_computation.1 | async-start | bytes 36765696 | tf_op jit(solution)/shard_map/all_gather | solution.py:97
  8.7 238.4 %all-gather.6.cloned.1.call-start = ((), (), s32[]{:S(2)}) async-start(), calls=%async_computation.2 | async-start | bytes 6127616 | tf_op jit(solution)/shard_map/all_gather | solution.py:102
  9.5 297.2 %all-gather.8.cloned.1.call-start = ((), (), s32[]{:S(2)}) async-start(), calls=%async_computation.3 | async-start | bytes 6127616 | tf_op jit(solution)/shard_map/all_gather | solution.py:107
  10.2 324.7 %all-reduce.7.cloned.1.call-start = ((), (), s32[]{:S(2)}) async-start(), calls=%async_computation.5 | async-start | bytes 147456 | tf_op jit(solution)/shard_map/psum | solution.py:59
  15.9 231.2 %copy-start.3 = (bf16[384,512]{1,0:T(8,128)(2,1)S(1)}, bf16[384,512]{1,0:T(8,128)(2,1)}, u32[]{:S(2)}) copy-start(bf16[384,512]{1,0:T(8,128)(2,1)} %param.22) | copy-start | bytes 1179652
  16.0 404.4 %reduce-scatter.2.cloned.1.call-start = ((), (), s32[]{:S(2)}) async-start(), calls=%async_computation.4 | async-start | bytes 12976128 | tf_op jit(solution)/shard_map/reduce_scatter | solution.py:109
  207.4 99.3 %copy-start.2 = (bf16[384,512]{1,0:T(8,128)(2,1)S(1)}, bf16[384,512]{1,0:T(8,128)(2,1)}, u32[]{:S(2)}) copy-start(bf16[384,512]{1,0:T(8,128)(2,1)} %param.23) | copy-start | bytes 1179652
  317.7 0.7 copy-start.5
  317.7 0.9 copy-start.6
  317.7 1.2 copy-start.4
  317.7 119.2 %all-reduce.9.cloned.1.call-start = ((), (), s32[]{:S(2)}) async-start(), calls=%async_computation.6 | async-start | bytes 131072 | tf_op jit(solution)/shard_map/psum | solution.py:88
  318.4 1.6 copy-start.1
  337.4 181.2 %all-reduce.11.cloned.1.call-start = ((), (), s32[]{:S(2)}) async-start(), calls=%async_computation.7 | async-start | bytes 1474560 | tf_op jit(solution)/shard_map/psum | solution.py:88
Sparse Core Ops, SparseCore 0:
  10.4 175.6 all-gather.3
  188.4 58.6 all-gather.5
  249.4 57.2 all-gather.7
  337.5 84.0 all-reduce.8
  425.5 93.0 all-reduce.10
Sparse Core Ops, SparseCore 1:
  16.0 23.3 all-reduce.6
  317.8 102.5 reduce-scatter.1
where the time goes:
time: 533 us; the launch traced here: 532 us
  waiting for transfers between devices  424 us (80%)
  matrix products  61.4 us (12%)
  blocking collectives  16 us (3%)
  between operations  15.3 us (3%)
  local copies, waits for them, and re-layouts  8.08 us (2%)
  other arithmetic  6.9 us (1%)
    all_gather x1, waiting for transfers between devices, shards(): lax.all_gather(query_projection_weight, 'fsdp', axis=0, tiled=True)  170 us
    reduce_scatter x1, waiting for transfers between devices, shards(): lax.psum_scatter(partial_back, 'tp', scatter_dimension=1, tiled=True)  81.6 us
    psum x2, waiting for transfers between devices, shards(): lax.psum((down_local, up_local[0], up_local[1], up_local[2]), 'fsdp')  81.6 us
    all_gather x1, waiting for transfers between devices, shards(): lax.all_gather(value_projection_weight, 'fsdp', axis=0, tiled=True)  48.7 us
    dot_general x3, matrix products, transposed_product(): lax.dot_general(cotangent, piece, (((1,), (1,)), ((), ())), preferred_ele...  43.2 us
    all_gather x1, waiting for transfers between devices, shards(): lax.all_gather(key_projection_weight, 'fsdp', axis=0, tiled=True)  39.7 us
    psum x1, blocking collectives, shards(): lax.psum((jnp.sum(token_width_matrix * token_width_matrix, axis=1), adapt...  11.1 us
  transfers between devices with their start and end apart: 7, of which 5 were waited for; matrix products, arithmetic and copies ran while one was open for 13% of the time, Pallas kernels for 0%

commit v1 on v0

v1 whole, which is shorter than its diff:
```python
import math

import jax
import jax.numpy as jnp
from jax import lax
from jax.sharding import PartitionSpec as P


norm_eps = 1e-05
adapter_scale = 2.0
late_shares = (0.5, 0.82)


def transposed_product(left, right):
    return lax.dot_general(
        left, right, (((1,), (1,)), ((), ())), preferred_element_type=jnp.float32
    )


def plain_back(weights, cotangents, full_width):
    total = jnp.zeros((cotangents[0].shape[0], full_width), jnp.float32)
    for weight, cotangent in zip(weights, cotangents):
        whole = lax.all_gather(weight, "fsdp", axis=0, tiled=True)
        total = total + transposed_product(cotangent, whole)
    return lax.psum_scatter(total, "tp", scatter_dimension=1, tiled=True)


def chunk_bounds(rows):
    cuts = [0] + [16 * int(rows * share / 16) for share in late_shares] + [rows]
    return [(low, high) for low, high in zip(cuts[:-1], cuts[1:])]


def grid_back(weights, cotangents, small_work):
    size = lax.axis_size("fsdp")
    top = size // 2
    place = lax.axis_index("fsdp")
    half = lax.axis_index("tp")

    def swap(value, bit):
        return lax.ppermute(value, "fsdp", [(i, i ^ bit) for i in range(size)])

    def cross(value, early):
        pairs = []
        for i in range(size):
            for t in range(2):
                if ((i // top) == t) != early:
                    pairs.append((2 * i + t, 2 * i + 1 - t))
        return lax.ppermute(value, ("fsdp", "tp"), pairs)

    cot = jnp.concatenate(cotangents, axis=1)
    weight = jnp.concatenate(weights, axis=1)
    rows = weight.shape[0]
    tokens_here = cot.shape[0]
    bounds = chunk_bounds(rows)

    cot_z = swap(cot, 4)
    far = [swap(weight[low:high], top) for low, high in bounds]
    weight_y = swap(weight, 2)
    cot_c = swap(cot, 1)
    mine = (place // top) == half

    def product(piece, cots):
        return transposed_product(piece, cots).astype(jnp.bfloat16)

    near_cot = jnp.concatenate([cot, cot_c], axis=0)
    early_weight = jnp.concatenate([weight, weight_y], axis=0)
    early = [product(early_weight, near_cot)]
    _, early[0], far[0] = lax.optimization_barrier((small_work, early[0], far[0]))
    early_got = [cross(early[0], True)]
    far_y = [swap(far[0], 2)]
    cot_zc = swap(cot_z, 1)
    far_cot = jnp.concatenate([cot_z, cot_zc], axis=0)
    early.append(product(early_weight, far_cot))
    early[1], far[1] = lax.optimization_barrier((early[1], far[1]))
    early_got.append(cross(early[1], True))
    far_y += [swap(far[index], 2) for index in range(1, len(bounds))]
    all_cot = jnp.concatenate([near_cot, far_cot], axis=0)
    late = [product(jnp.concatenate(pair, axis=0), all_cot) for pair in zip(far, far_y)]
    late_got = [cross(part, False) for part in late]

    def add(a, b):
        return a.astype(jnp.float32) + b.astype(jnp.float32)

    blocks = [[None] * len(bounds) for _ in range(8)]
    for index, (low, high) in enumerate(bounds):
        depth = high - low
        l = add(late[index], late_got[index]).reshape(2, depth, -1)
        sums = []
        for side in range(2):
            e = add(early[side], early_got[side]).reshape(2, rows, -1)[:, low:high]
            l_side = l[..., 2 * tokens_here * side : 2 * tokens_here * (side + 1)]
            sums.append(jnp.where(mine, e, l_side).astype(jnp.bfloat16))
        near, far_sum = sums
        got = swap(far_sum, 4)
        send = jnp.concatenate([near[..., tokens_here:], got[..., tokens_here:]], axis=2)
        other = swap(send, 1)
        four = (
            near[..., :tokens_here],
            other[..., :tokens_here],
            got[..., :tokens_here],
            other[..., tokens_here:],
        )
        for relative, block in zip((0, 1, 4, 5), four):
            for member in range(2):
                blocks[relative ^ (2 * member)][index] = block[member]
    result = jnp.stack([jnp.concatenate(parts, axis=0) for parts in blocks])
    base = place % top
    for bit in (1, 2, 4):
        pair = result.reshape(8 // (2 * bit), 2, bit, rows, tokens_here)
        result = jnp.where((base // bit) % 2 == 1, pair[:, ::-1], pair)
    result = result.reshape(top * rows, tokens_here)
    return result.T.astype(jnp.float32)


def shards(
    tokens,
    gain,
    query_projection_weight,
    key_projection_weight,
    value_projection_weight,
    adapter_down_factors,
    query_adapter_up,
    key_adapter_up,
    value_adapter_up,
    query_cotangent,
    key_cotangent,
    value_cotangent,
):
    return device_work(
        tokens,
        gain,
        (query_projection_weight, key_projection_weight, value_projection_weight),
        adapter_down_factors,
        (query_adapter_up, key_adapter_up, value_adapter_up),
        (query_cotangent, key_cotangent, value_cotangent),
    )


def device_work(tokens, gain, weights, adapter_down_factors, ups, cots):
    fsdp_size = lax.axis_size("fsdp")
    tp_size = lax.axis_size("tp")
    tp_index = lax.axis_index("tp")
    row_count, owned = tokens.shape
    full_width = gain.shape[0]
    rank = adapter_down_factors.shape[1]

    def tp_sum(value):
        if tp_size != 2:
            return lax.psum(value, "tp")
        return value + lax.ppermute(value, "tp", [(0, 1), (1, 0)])

    wide = tokens.astype(jnp.float32)
    gain_own = lax.dynamic_slice_in_dim(gain, tp_index * owned, owned, 0)
    down = lax.dynamic_slice_in_dim(adapter_down_factors, tp_index * owned, owned, 2)
    down = down.reshape(3 * rank, owned)
    low_in = lax.dot_general(
        wide * gain_own[None, :],
        down.astype(jnp.float32),
        (((1,), (1,)), ((), ())),
        precision=lax.Precision.HIGHEST,
    )
    low_out = jnp.concatenate([transposed_product(c, u) for c, u in zip(cots, ups)], axis=1)
    squares = jnp.sum(wide * wide, axis=1, keepdims=True)
    small = tp_sum(jnp.concatenate([squares, low_in, low_out], axis=1))
    inverse = lax.rsqrt(small[:, :1] / full_width + norm_eps)
    in_low = (small[:, 1 : 1 + 3 * rank] * inverse).astype(jnp.bfloat16)
    out_low = small[:, 1 + 3 * rank :].astype(jnp.bfloat16)
    unit_rows = wide * inverse
    normed = (unit_rows * gain_own[None, :]).astype(jnp.bfloat16)
    scale = adapter_scale / math.sqrt(row_count * fsdp_size)

    def token_product(left, right):
        return scale * lax.dot_general(
            left, right, (((0,), (0,)), ((), ())), preferred_element_type=jnp.float32
        )

    down_local = token_product(out_low, normed)
    up_local = [
        token_product(in_low[:, rank * m : rank * (m + 1)], cots[m]) for m in range(3)
    ]
    small_work = tuple(down_local[rank * m : rank * (m + 1)] for m in range(3)) + tuple(up_local)
    if tp_size == 2 and fsdp_size == 16:
        back = grid_back(weights, cots, small_work)
    else:
        back = plain_back(weights, cots, full_width)
    grads = lax.psum(jnp.concatenate(small_work, axis=1), "fsdp")
    grad_down = jnp.stack([grads[:, owned * m : owned * (m + 1)] for m in range(3)])
    ends = [3 * owned]
    for cot in cots:
        ends.append(ends[-1] + cot.shape[1])
    up_q, up_k, up_v = [grads[:, low:high] for low, high in zip(ends[:-1], ends[1:])]

    back = back + adapter_scale * jnp.dot(out_low, down, preferred_element_type=jnp.float32)
    gained = gain_own[None, :] * back
    inner = tp_sum(jnp.sum(gained * unit_rows, axis=1, keepdims=True)) / full_width
    grad_tokens = (inverse * (gained - unit_rows * inner)).astype(jnp.bfloat16)
    return (grad_tokens, grad_down, up_q, up_k, up_v)


def solution(mesh):
    in_specs = (
        P("fsdp", "tp"),
        P(),
        P("fsdp", "tp"),
        P("fsdp", "tp"),
        P("fsdp", "tp"),
        P(),
        P(None, "tp"),
        P(None, "tp"),
        P(None, "tp"),
        P("fsdp", "tp"),
        P("fsdp", "tp"),
        P("fsdp", "tp"),
    )
    out_specs = (P("fsdp", "tp"), P(None, None, "tp"), P(None, "tp"), P(None, "tp"), P(None, "tp"))
    return jax.shard_map(shards, mesh=mesh, in_specs=in_specs, out_specs=out_specs, check_vma=False)
```

time: 533 us -> 380 us (0.71)
  waiting for transfers between devices: 424 us -> 238 us
  starting transfers between devices: 0.46 us -> 34.9 us
  local copies, waits for them, and re-layouts: 8.08 us -> 30.2 us
  blocking collectives: 16 us -> 0 us
  matrix products: 61.4 us -> 52.3 us
    all_gather x3 -> x0, waiting for transfers between devices: 258 us -> none  [the longest x1 170 us: shards(): lax.all_gather(query_projection_weight, 'fsdp', axis=0, tiled=True)]
    ppermute x0 -> x23, waiting for transfers between devices: none -> 131 us  [the longest x16 122 us: swap(): return lax.ppermute(value, 'fsdp', [(i, i ^ bit) for i in range(size)])]
    reduce_scatter x1 -> x0, waiting for transfers between devices: 81.6 us -> none  [shards(): lax.psum_scatter(partial_back, 'tp', scatter_dimension=1, tiled=True)]
    ppermute x0 -> x23, starting transfers between devices: none -> 34.9 us  [the longest x16 17.6 us: swap(): return lax.ppermute(value, 'fsdp', [(i, i ^ bit) for i in range(size)])]
    psum x3 -> x1, waiting for transfers between devices: 81.6 us -> 107 us  [device_work(): grads = lax.psum(jnp.concatenate(small_work, axis=1), 'fsdp')]
    psum x2 -> x0, blocking collectives: 16 us -> none  [the longest x1 11.1 us: shards(): lax.psum((jnp.sum(token_width_matrix * token_width_matrix, axis=1), adapt...]
    slice x0 -> x11, local copies, waits for them, and re-layouts: none -> 9.82 us  [the longest x3 6.68 us: grid_back(): far = [swap(weight[low:high], top) for low, high in bounds]]
    dot_general x12 -> x14, matrix products: 61.4 us -> 52.3 us  [the longest x8 42.7 us: transposed_product(): lax.dot_general(left, right, (((1,), (1,)), ((), ())), preferred_element_...]
  transfers between devices with their start and end apart: 7 -> 24, of which waited for: 5 -> 11; matrix products, arithmetic and copies ran while one was open for 13% -> 19% of each run, Pallas kernels for 0% -> 0%
where the time goes in v1:
time: 380 us; the launch traced here: 379 us
  waiting for transfers between devices  238 us (63%)
  matrix products  52.3 us (14%)
  starting transfers between devices  34.9 us (9%)
  local copies, waits for them, and re-layouts  30.2 us (8%)
  between operations  14.6 us (4%)
  other arithmetic  9.7 us (3%)
    ppermute x16, waiting for transfers between devices, swap(): return lax.ppermute(value, 'fsdp', [(i, i ^ bit) for i in range(size)])  122 us
    psum x1, waiting for transfers between devices, device_work(): grads = lax.psum(jnp.concatenate(small_work, axis=1), 'fsdp')  107 us
    dot_general x8, matrix products, transposed_product(): lax.dot_general(left, right, (((1,), (1,)), ((), ())), preferred_element_...  42.7 us
    ppermute x16, starting transfers between devices, swap(): return lax.ppermute(value, 'fsdp', [(i, i ^ bit) for i in range(size)])  17.6 us
    ppermute x5, starting transfers between devices, cross(): return lax.ppermute(value, ('fsdp', 'tp'), pairs)  13.2 us
    unnamed x47, local copies, waits for them, and re-layouts  10.8 us
    ppermute x5, waiting for transfers between devices, cross(): return lax.ppermute(value, ('fsdp', 'tp'), pairs)  8.47 us
  transfers between devices with their start and end apart: 24, of which 11 were waited for; matrix products, arithmetic and copies ran while one was open for 19% of the time, Pallas kernels for 0%

profile of v1, /device:TPU:0, one launch (start us, length us, event | category | flops | bytes accessed | tf_op | source)
XLA Modules:
  0.0 379.3 jit_solution(10266697251575392782)
XLA Ops:
  7.3 3.4 constant_dynamic-update-slice_fusion.5
  12.3 3.1 collective-permute-start.6
  17.7 2.5 fusion.19
  22.4 3.1 constant_dynamic-update-slice_fusion.2
  28.7 1.9 slice.295
  30.6 2.6 collective-permute-start.12
  33.1 2.6 slice.286
  39.1 86.8 %collective-permute-done.6 = bf16[384,4096]{1,0:T(8,128)(2,1)} collective-permute-done((bf16[384,4096]{1,0:T(8,128)(2,1)}, bf16[384,4096]{1,0:T(8,128)(2,1)}, u32[]{:S(2)}, u32[]{:S(2)}) %collective-permute-start.6) | collective-permute-done | bytes 3145760 | tf_op jit(solution)/shard_map/ppermute | solution.py:40
  128.6 9.2 %fusion.37 = bf16[704,768]{1,0:T(8,128)(2,1)S(1)} fusion(bf16[384,4096]{1,0:T(8,128)(2,1)} %collective-permute-done.2, bf16[384,4096]{1,0:T(8,128)(2,1)} %constant_dynamic-update-slice_fusion.3, bf16[352,4096]{1,0:T(8,128)(2,1)} %collective-permute-done.1, bf16[352,4096]{1,0:T(8,128)(2,1)} %constant_dynamic-update-slice_fusion), kind=kOutput, calls=%fused_computation.49 | convolution fusion | flops 4453842944 | bytes 13139968 | tf_op jit(solution)/shard_map/dot_general | solution.py:15
  139.3 2.2 slice.291
  141.5 4.0 %collective-permute-start.9 = (bf16[112,4096]{1,0:T(8,128)(2,1)}, bf16[112,4096]{1,0:T(8,128)(2,1)}, u32[]{:S(2)}, u32[]{:S(2)}) collective-permute-start(bf16[112,4096]{1,0:T(8,128)(2,1)} %slice.291), channel_id=1, source_target_pairs={{0,16},{2,18},{4,20},{6,22},{8,24},{10,26},{12,28},{14,30},{16,0},... | collective-permute-start | bytes 2752520 | tf_op jit(solution)/shard_map/ppermute | solution.py:40
  147.0 106.9 %all-reduce.2.cloned.1.call-done = f32[16,12544]{1,0:T(8,128)} async-done(((f32[16,12544]{1,0:T(8,128)}), f32[16,12544]{1,0:T(8,128)}) %all-reduce.2.cloned.1.call-update) | async-done | bytes 802832 | tf_op jit(solution)/shard_map/psum | solution.py:186
  257.2 7.4 %convolution_convert_fusion.1 = bf16[128,1536]{1,0:T(8,128)(2,1)S(1)} fusion(bf16[64,4096]{1,0:T(8,128)(2,1)S(1)} %collective-permute-done.13, bf16[64,4096]{1,0:T(8,128)(2,1)} %collective-permute-done.12, bf16[384,4096]{1,0:T(8,128)(2,1)} %collective-permute-done.7, bf16[384,4096]{1,0:T(8,128)(2,1)} %collective-permute-done.6, ...), kind=kOutput, calls=%fused_computation.37 | convolution fusion | flops 1663238144 | bytes 14024704 | tf_op jit(solution)/shard_map/dot_general | solution.py:15
  264.7 3.4 collective-permute-start.14
  268.1 9.2 %fusion.34 = bf16[704,768]{1,0:T(8,128)(2,1)S(1)} fusion(bf16[384,4096]{1,0:T(8,128)(2,1)} %collective-permute-done.7, bf16[384,4096]{1,0:T(8,128)(2,1)} %collective-permute-done.6, bf16[352,4096]{1,0:T(8,128)(2,1)} %collective-permute-done.1, bf16[352,4096]{1,0:T(8,128)(2,1)} %constant_dynamic-update-slice_fusion), kind=kOutput, calls=%fused_computation.48 | convolution fusion | flops 4453842944 | bytes 13139968 | tf_op jit(solution)/shard_map/dot_general | solution.py:15
  279.6 11.0 %collective-permute-done.5 = bf16[176,4096]{1,0:T(8,128)(2,1)S(1)} collective-permute-done((bf16[176,4096]{1,0:T(8,128)(2,1)}, bf16[176,4096]{1,0:T(8,128)(2,1)S(1)}, u32[]{:S(2)}, u32[]{:S(2)}) %collective-permute-start.5) | collective-permute-done | bytes 1441824 | tf_op jit(solution)/shard_map/ppermute | solution.py:40
  290.6 8.5 %fusion.24 = bf16[352,1536]{1,0:T(8,128)(2,1)S(1)} fusion(bf16[176,4096]{1,0:T(8,128)(2,1)S(1)} %collective-permute-done.5, bf16[176,4096]{1,0:T(8,128)(2,1)} %collective-permute-done.3, bf16[384,4096]{1,0:T(8,128)(2,1)} %collective-permute-done.7, bf16[384,4096]{1,0:T(8,128)(2,1)} %collective-permute-done.6, bf16[384,4096]{1,0:T(8,128)(2,1)} %collective-permute-done.2, ...), kind=kOutput, calls=%fused_computation.35 | convolution fusion | flops 4485824512 | bytes 16547840 | tf_op jit(solution)/shard_map/dot_general | solution.py:15
  299.1 3.4 collective-permute-start.8
  302.6 7.0 %collective-permute-done.10 = bf16[112,4096]{1,0:T(8,128)(2,1)} collective-permute-done((bf16[112,4096]{1,0:T(8,128)(2,1)}, bf16[112,4096]{1,0:T(8,128)(2,1)}, u32[]{:S(2)}, u32[]{:S(2)}) %collective-permute-start.10) | collective-permute-done | bytes 917536 | tf_op jit(solution)/shard_map/ppermute | solution.py:40
  309.7 7.3 %convolution_convert_fusion = bf16[224,1536]{1,0:T(8,128)(2,1)S(1)} fusion(bf16[112,4096]{1,0:T(8,128)(2,1)} %collective-permute-done.10, bf16[112,4096]{1,0:T(8,128)(2,1)} %collective-permute-done.9, bf16[384,4096]{1,0:T(8,128)(2,1)} %collective-permute-done.7, bf16[384,4096]{1,0:T(8,128)(2,1)} %collective-permute-done.6, ...), kind=kOutput, calls=%fused_computation.36 | convolution fusion | flops 2872918016 | bytes 15106048 | tf_op jit(solution)/shard_map/dot_general | solution.py:15
  317.0 3.6 collective-permute-start.11
  321.0 5.7 %collective-permute-done.8 = bf16[352,1536]{1,0:T(8,128)(2,1)S(1)} collective-permute-done((bf16[352,1536]{1,0:T(8,128)(2,1)S(1)}, bf16[352,1536]{1,0:T(8,128)(2,1)S(1)}, u32[]{:S(2)}, u32[]{:S(2)}) %collective-permute-start.8) | collective-permute-done | bytes 1081376 | tf_op jit(solution)/shard_map/ppermute | solution.py:48
  329.4 5.6 %collective-permute-done.20 = bf16[2,64,768]{2,1,0:T(8,128)(2,1)S(1)} collective-permute-done((bf16[2,64,768]{2,1,0:T(8,128)(2,1)S(1)}, bf16[2,64,768]{2,1,0:T(8,128)(2,1)S(1)}, u32[]{:S(2)}, u32[]{:S(2)}) %collective-permute-start.20) | collective-permute-done | bytes 196640 | tf_op jit(solution)/shard_map/ppermute | solution.py:40
  336.6 2.7 collective-permute-done.11
  339.7 2.8 collective-permute-done.16
  342.8 6.0 %collective-permute-done.18 = bf16[2,112,768]{2,1,0:T(8,128)(2,1)S(1)} collective-permute-done((bf16[2,112,768]{2,1,0:T(8,128)(2,1)S(1)}, bf16[2,112,768]{2,1,0:T(8,128)(2,1)S(1)}, u32[]{:S(2)}, u32[]{:S(2)}) %collective-permute-start.18) | collective-permute-done | bytes 344096 | tf_op jit(solution)/shard_map/ppermute | solution.py:40
  352.3 2.6 bitcast_convert_fusion
  354.8 5.9 %copy.19 = f32[2816,384]{0,1:T(8,128)} copy(f32[2816,384]{1,0:T(8,128)} %bitcast_convert_fusion) | data formatting | bytes 8650752 | tf_op jit(solution)/shard_map/convert_element_type | solution.py:112
  360.7 3.6 fusion.14
  364.3 2.5 collective-permute-start.22
  368.3 1.6 slice.334
  369.9 2.6 fusion.17
  (137 shorter events, 33.9 us)
Async XLA Ops:
  7.2 8.7 %copy-start = (bf16[3,16,5632]{2,1,0:T(8,128)(2,1)S(1)}, bf16[3,16,5632]{2,1,0:T(8,128)(2,1)}, u32[]{:S(2)}) copy-start(bf16[3,16,5632]{2,1,0:T(8,128)(2,1)} %param.17) | copy-start | bytes 1622020
  7.2 246.7 %all-reduce.2.cloned.1.call-start = ((), (), s32[]{:S(2)}) async-start(), calls=%async_computation | async-start | bytes 1605632 | tf_op jit(solution)/shard_map/psum | solution.py:186
  7.2 8.1 %copy-start.3 = (bf16[384,2816]{1,0:T(8,128)(2,1)S(1)}, bf16[384,2816]{1,0:T(8,128)(2,1)}, u32[]{:S(2)}) copy-start(bf16[384,2816]{1,0:T(8,128)(2,1)} %param.12) | copy-start | bytes 6488068
  12.3 113.6 %collective-permute-start.6 = (bf16[384,4096]{1,0:T(8,128)(2,1)}, bf16[384,4096]{1,0:T(8,128)(2,1)}, u32[]{:S(2)}, u32[]{:S(2)}) collective-permute-start(bf16[384,4096]{1,0:T(8,128)(2,1)} %constant_dynamic-update-slice_fusion.3), channel_id=1, source_target_pairs={{0,8},{2,10},{4,12},{6,14},{8,0},{10,2},{12,4},{14,6},{16,24},{18,... | collective-permute-start | bytes 9437192 | tf_op jit(solution)/shard_map/ppermute | solution.py:40
  15.3 113.3 %collective-permute-start.2 = (bf16[384,4096]{1,0:T(8,128)(2,1)}, bf16[384,4096]{1,0:T(8,128)(2,1)}, u32[]{:S(2)}, u32[]{:S(2)}) collective-permute-start(bf16[384,4096]{1,0:T(8,128)(2,1)} %constant_dynamic-update-slice_fusion.3), channel_id=1, source_target_pairs={{0,2},{2,0},{4,6},{6,4},{8,10},{10,8},{12,14},{14,12},{16,18},{18,... | collective-permute-start | bytes 9437192 | tf_op jit(solution)/shard_map/ppermute | solution.py:40
  17.7 7.8 %copy-start.14 = (bf16[352,512]{1,0:T(8,128)(2,1)S(1)}, bf16[352,512]{1,0:T(8,128)(2,1)}, u32[]{:S(2)}) copy-start(bf16[352,512]{1,0:T(8,128)(2,1)} %param.15) | copy-start | bytes 1081348
  20.8 14.9 %collective-permute-start = (f32[384,97]{0,1:T(8,128)S(1)}, f32[384,97]{0,1:T(8,128)S(1)}, u32[]{:S(2)}, u32[]{:S(2)}) collective-permute-start(f32[384,97]{0,1:T(8,128)S(1)} %concatenate.67), channel_id=1, source_target_pairs={{0,1},{1,0},{2,3},{3,2},{4,5},{5,4},{6,7},{7,6},{8,9},{9,8},{10,11... | collective-permute-start | bytes 446984 | tf_op jit(solution)/shard_map/ppermute | solution.py:150
  25.5 10.7 %copy-start.5 = (bf16[384,2816]{1,0:T(8,128)(2,1)S(1)}, bf16[384,2816]{1,0:T(8,128)(2,1)}, u32[]{:S(2)}) copy-start(bf16[384,2816]{1,0:T(8,128)(2,1)} %param.12) | copy-start | bytes 6488068
  27.1 101.5 %collective-permute-start.1 = (bf16[352,4096]{1,0:T(8,128)(2,1)}, bf16[352,4096]{1,0:T(8,128)(2,1)}, u32[]{:S(2)}, u32[]{:S(2)}) collective-permute-start(bf16[352,4096]{1,0:T(8,128)(2,1)} %constant_dynamic-update-slice_fusion), channel_id=1, source_target_pairs={{0,4},{2,6},{4,0},{6,2},{8,12},{10,14},{12,8},{14,10},{16,20},{18,... | collective-permute-start | bytes 8650760 | tf_op jit(solution)/shard_map/ppermute | solution.py:40
  30.6 114.9 %collective-permute-start.12 = (bf16[64,4096]{1,0:T(8,128)(2,1)}, bf16[64,4096]{1,0:T(8,128)(2,1)}, u32[]{:S(2)}, u32[]{:S(2)}) collective-permute-start(bf16[64,4096]{1,0:T(8,128)(2,1)} %slice.295), channel_id=1, source_target_pairs={{0,16},{2,18},{4,20},{6,22},{8,24},{10,26},{12,28},{14,30},{16,0},... | collective-permute-start | bytes 1572872 | tf_op jit(solution)/shard_map/ppermute | solution.py:40
  35.8 102.0 %collective-permute-start.3 = (bf16[176,4096]{1,0:T(8,128)(2,1)}, bf16[176,4096]{1,0:T(8,128)(2,1)}, u32[]{:S(2)}, u32[]{:S(2)}) collective-permute-start(bf16[176,4096]{1,0:T(8,128)(2,1)} %slice.286), channel_id=1, source_target_pairs={{0,16},{2,18},{4,20},{6,22},{8,24},{10,26},{12,28},{14,30},{16,0},... | collective-permute-start | bytes 4325384 | tf_op jit(solution)/shard_map/ppermute | solution.py:40
  36.1 90.9 %copy-start.13 = (f32[384,97]{0,1:T(8,128)}, f32[384,97]{0,1:T(8,128)S(1)}, u32[]{:S(2)}) copy-start(f32[384,97]{0,1:T(8,128)S(1)} %add.58) | copy-start | bytes 446980
  37.0 90.8 %copy-start.10 = (bf16[384,512]{1,0:T(8,128)(2,1)S(1)}, bf16[384,512]{1,0:T(8,128)(2,1)}, u32[]{:S(2)}) copy-start(bf16[384,512]{1,0:T(8,128)(2,1)} %param.23) | copy-start | bytes 1179652
  125.9 131.3 %collective-permute-start.7 = (bf16[384,4096]{1,0:T(8,128)(2,1)}, bf16[384,4096]{1,0:T(8,128)(2,1)}, u32[]{:S(2)}, u32[]{:S(2)}) collective-permute-start(bf16[384,4096]{1,0:T(8,128)(2,1)} %collective-permute-done.6), channel_id=1, source_target_pairs={{0,2},{2,0},{4,6},{6,4},{8,10},{10,8},{12,14},{14,12},{16,18},{18,... | collective-permute-start | bytes 9437192 | tf_op jit(solution)/shard_map/ppermute | solution.py:40
  137.8 119.2 %collective-permute-start.4 = (bf16[704,768]{1,0:T(8,128)(2,1)S(1)}, bf16[704,768]{1,0:T(8,128)(2,1)S(1)}, u32[]{:S(2)}, u32[]{:S(2)}) collective-permute-start(bf16[704,768]{1,0:T(8,128)(2,1)S(1)} %fusion.37), channel_id=1, source_target_pairs={{1,0},{3,2},{5,4},{7,6},{9,8},{11,10},{13,12},{15,14},{16,17},{18,... | collective-permute-start | bytes 3244040 | tf_op jit(solution)/shard_map/ppermute | solution.py:48
  141.5 135.8 %collective-permute-start.9 = (bf16[112,4096]{1,0:T(8,128)(2,1)}, bf16[112,4096]{1,0:T(8,128)(2,1)}, u32[]{:S(2)}, u32[]{:S(2)}) collective-permute-start(bf16[112,4096]{1,0:T(8,128)(2,1)} %slice.291), channel_id=1, source_target_pairs={{0,16},{2,18},{4,20},{6,22},{8,24},{10,26},{12,28},{14,30},{16,0},... | collective-permute-start | bytes 2752520 | tf_op jit(solution)/shard_map/ppermute | solution.py:40
  145.5 111.7 %collective-permute-start.13 = (bf16[64,4096]{1,0:T(8,128)(2,1)}, bf16[64,4096]{1,0:T(8,128)(2,1)S(1)}, u32[]{:S(2)}, u32[]{:S(2)}) collective-permute-start(bf16[64,4096]{1,0:T(8,128)(2,1)} %collective-permute-done.12), channel_id=1, source_target_pairs={{0,4},{2,6},{4,0},{6,2},{8,12},{10,14},{12,8},{14,10},{16,20},{18,... | collective-permute-start | bytes 1572872 | tf_op jit(solution)/shard_map/ppermute | solution.py:40
  255.9 34.7 %collective-permute-start.5 = (bf16[176,4096]{1,0:T(8,128)(2,1)}, bf16[176,4096]{1,0:T(8,128)(2,1)S(1)}, u32[]{:S(2)}, u32[]{:S(2)}) collective-permute-start(bf16[176,4096]{1,0:T(8,128)(2,1)} %collective-permute-done.3), channel_id=1, source_target_pairs={{0,4},{2,6},{4,0},{6,2},{8,12},{10,14},{12,8},{14,10},{16,20},{18,... | collective-permute-start | bytes 4325384 | tf_op jit(solution)/shard_map/ppermute | solution.py:40
  264.7 37.9 %collective-permute-start.14 = (bf16[128,1536]{1,0:T(8,128)(2,1)S(1)}, bf16[128,1536]{1,0:T(8,128)(2,1)S(1)}, u32[]{:S(2)}, u32[]{:S(2)}) collective-permute-start(bf16[128,1536]{1,0:T(8,128)(2,1)S(1)} %convolution_convert_fusion.1), channel_id=1, source_target_pairs={{0,1},{2,3},{4,5},{6,7},{8,9},{10,11},{12,13},{14,15},{17,16},{19,... | collective-permute-start | bytes 1179656 | tf_op jit(solution)/shard_map/ppermute | solution.py:48
  277.3 43.3 %collective-permute-start.15 = (bf16[704,768]{1,0:T(8,128)(2,1)S(1)}, bf16[704,768]{1,0:T(8,128)(2,1)S(1)}, u32[]{:S(2)}, u32[]{:S(2)}) collective-permute-start(bf16[704,768]{1,0:T(8,128)(2,1)S(1)} %fusion.34), channel_id=1, source_target_pairs={{1,0},{3,2},{5,4},{7,6},{9,8},{11,10},{13,12},{15,14},{16,17},{18,... | collective-permute-start | bytes 3244040 | tf_op jit(solution)/shard_map/ppermute | solution.py:48
  278.6 31.1 %collective-permute-start.10 = (bf16[112,4096]{1,0:T(8,128)(2,1)}, bf16[112,4096]{1,0:T(8,128)(2,1)}, u32[]{:S(2)}, u32[]{:S(2)}) collective-permute-start(bf16[112,4096]{1,0:T(8,128)(2,1)} %collective-permute-done.9), channel_id=1, source_target_pairs={{0,4},{2,6},{4,0},{6,2},{8,12},{10,14},{12,8},{14,10},{16,20},{18,... | collective-permute-start | bytes 2752520 | tf_op jit(solution)/shard_map/ppermute | solution.py:40
  299.1 27.6 %collective-permute-start.8 = (bf16[352,1536]{1,0:T(8,128)(2,1)S(1)}, bf16[352,1536]{1,0:T(8,128)(2,1)S(1)}, u32[]{:S(2)}, u32[]{:S(2)}) collective-permute-start(bf16[352,1536]{1,0:T(8,128)(2,1)S(1)} %fusion.24), channel_id=1, source_target_pairs={{0,1},{2,3},{4,5},{6,7},{8,9},{10,11},{12,13},{14,15},{17,16},{19,... | collective-permute-start | bytes 3244040 | tf_op jit(solution)/shard_map/ppermute | solution.py:48
  317.0 22.3 %collective-permute-start.11 = (bf16[224,1536]{1,0:T(8,128)(2,1)S(1)}, bf16[224,1536]{1,0:T(8,128)(2,1)S(1)}, u32[]{:S(2)}, u32[]{:S(2)}) collective-permute-start(bf16[224,1536]{1,0:T(8,128)(2,1)S(1)} %convolution_convert_fusion), channel_id=1, source_target_pairs={{0,1},{2,3},{4,5},{6,7},{8,9},{10,11},{12,13},{14,15},{17,16},{19,... | collective-permute-start | bytes 2064392 | tf_op jit(solution)/shard_map/ppermute | solution.py:48
  327.1 7.8 %collective-permute-start.20 = (bf16[2,64,768]{2,1,0:T(8,128)(2,1)S(1)}, bf16[2,64,768]{2,1,0:T(8,128)(2,1)S(1)}, u32[]{:S(2)}, u32[]{:S(2)}) collective-permute-start(bf16[2,64,768]{2,1,0:T(8,128)(2,1)S(1)} %get-tuple-element.30), channel_id=1, source_target_pairs={{0,8},{2,10},{4,12},{6,14},{8,0},{10,2},{12,4},{14,6},{16,24},{18,... | collective-permute-start | bytes 589832 | tf_op jit(solution)/shard_map/ppermute | solution.py:40
  327.8 14.8 %collective-permute-start.16 = (bf16[2,176,768]{2,1,0:T(8,128)(2,1)S(1)}, bf16[2,176,768]{2,1,0:T(8,128)(2,1)S(1)}, u32[]{:S(2)}, u32[]{:S(2)}) collective-permute-start(bf16[2,176,768]{2,1,0:T(8,128)(2,1)S(1)} %get-tuple-element.13), channel_id=1, source_target_pairs={{0,8},{2,10},{4,12},{6,14},{8,0},{10,2},{12,4},{14,6},{16,24},{18,... | collective-permute-start | bytes 1622024 | tf_op jit(solution)/shard_map/ppermute | solution.py:40
  335.0 1.5 collective-permute-start.21
  339.5 9.2 %collective-permute-start.18 = (bf16[2,112,768]{2,1,0:T(8,128)(2,1)S(1)}, bf16[2,112,768]{2,1,0:T(8,128)(2,1)S(1)}, u32[]{:S(2)}, u32[]{:S(2)}) collective-permute-start(bf16[2,112,768]{2,1,0:T(8,128)(2,1)S(1)} %get-tuple-element.20), channel_id=1, source_target_pairs={{0,8},{2,10},{4,12},{6,14},{8,0},{10,2},{12,4},{14,6},{16,24},{18,... | collective-permute-start | bytes 1032200 | tf_op jit(solution)/shard_map/ppermute | solution.py:40
  342.6 6.2 %collective-permute-start.17 = (bf16[2,176,768]{2,1,0:T(8,128)(2,1)S(1)}, bf16[2,176,768]{2,1,0:T(8,128)(2,1)S(1)}, u32[]{:S(2)}, u32[]{:S(2)}) collective-permute-start(bf16[2,176,768]{2,1,0:T(8,128)(2,1)S(1)} %pad_maximum_fusion.8), channel_id=1, source_target_pairs={{0,2},{2,0},{4,6},{6,4},{8,10},{10,8},{12,14},{14,12},{16,18},{18,... | collective-permute-start | bytes 1622024 | tf_op jit(solution)/shard_map/ppermute | solution.py:40
  348.8 1.7 collective-permute-start.19
  354.8 5.9 %copy-start.6 = (bf16[384,2816]{1,0:T(8,128)(2,1)S(1)}, bf16[384,2816]{1,0:T(8,128)(2,1)}, u32[]{:S(2)}) copy-start(bf16[384,2816]{1,0:T(8,128)(2,1)} %param.12) | copy-start | bytes 6488068
  354.8 5.9 %copy-start.12 = (bf16[3,16,2816]{2,1,0:T(8,128)(2,1)S(1)}, bf16[3,16,2816]{2,1,0:T(8,128)(2,1)}, u32[]{:S(2)}) copy-start(bf16[3,16,2816]{2,1,0:T(8,128)(2,1)} %copy-done.11) | copy-start | bytes 811012
  364.3 5.6 %collective-permute-start.22 = (f32[384,1]{0,1:T(1,128)S(1)}, f32[384,1]{0,1:T(1,128)S(1)}, u32[]{:S(2)}, u32[]{:S(2)}) collective-permute-start(f32[384,1]{0,1:T(1,128)S(1)} %broadcast_in_dim.10), channel_id=1, source_target_pairs={{0,1},{1,0},{2,3},{3,2},{4,5},{5,4},{6,7},{7,6},{8,9},{9,8},{10,11... | collective-permute-start | bytes 4616 | tf_op jit(solution)/shard_map/ppermute | solution.py:150
  (12 other events, 42.1 us)
Sparse Core Ops, SparseCore 0:
  128.7 125.1 all-reduce.1
